TPU v7x, 128 devices: a whole 4x4x4 slice. The times are simulated.
128 devices in a mesh: ep: 32 (over z, x, core), dp: 4 (over y).
Axes of the slice: x: 4, y: 4, z: 4, core: 2. Of those that a mesh axis runs over, the one named last changes fastest.
Arguments:
- grad_out: float32 [16384, 1536], P(('ep', 'dp')), may hold values from -6 to 6
- tokens: bfloat16 [16384, 1536], P(('ep', 'dp')), may hold values from -6 to 6
- probs: float32 [16384, 4], P(('ep', 'dp')), may hold values from 0.1 to 0.5
- expert_ids: int32 [16384, 4], P(('ep', 'dp')), may hold values from 0 to 31, all different within a row; in each aligned block of 128 rows (0 to 127, 128 to 255, ...) at most 20 rows name the same one
- priority: int32 [128, 128], P(('ep', 'dp')), may hold values from 0 to 127, each once within a row
- cap_counts: int32 [32], replicated, may hold values from 10 to 20, as said below
- gate_weight: bfloat16 [32, 1536, 1536], P('ep'), may hold values from -0.15625 to 0.15625
- up_weight: bfloat16 [32, 1536, 1536], P('ep'), may hold values from -0.15625 to 0.15625
- down_weight: bfloat16 [32, 1536, 1536], P('ep'), may hold values from -0.15625 to 0.15625
Outputs:
- input_grad: bfloat16 [16384, 1536], P(('ep', 'dp'))
- prob_grad: float32 [16384, 4], P(('ep', 'dp'))
- gate_grad: bfloat16 [32, 1536, 1536], P('ep', 'dp')
- up_grad: bfloat16 [32, 1536, 1536], P('ep', 'dp')
- down_grad: bfloat16 [32, 1536, 1536], P('ep', 'dp')
Inputs may be any that keep to these rules, and one draw needn't show every extreme that they name: `expert_ids`: each row names 4 different experts; among the rows of one device no expert is named by more than 20 rows, and in some device some expert is named by exactly 20 rows. `priority`: each row orders the 128 tokens of one device, each number once. `cap_counts`: some expert has exactly 20.
All inputs are finite; a program needn't handle non-finite values. Where the computation divides by a largest or mean magnitude, that divisor is 1e-20 or more.
Results may differ from a plain program's by a relative error of at most 0.017.
Values may be sent and summed in bfloat16 or wider, within the bound.
A program may use at most 128 MiB of HBM per device.

v0:
```python
import jax
import jax.numpy as jnp
from jax import lax
from jax.sharding import PartitionSpec as P

sharpness = 1.702


def shortened(array):

    def short(part):
        return part.astype(jnp.bfloat16) if part.dtype == jnp.float32 else part

    return jax.tree.map(short, array)


def contract_last(first_op, second_op):
    return lax.dot_general(
        first_op, second_op, (((1,), (1,)), ((), ())), preferred_element_type=jnp.float32
    )


def contract_first(first_op, second_op):
    return lax.dot_general(
        first_op, second_op, (((0,), (0,)), ((), ())), preferred_element_type=jnp.float32
    )


def route_table(expert_ids, priority, cap_counts, buckets, capacity):
    ranking = priority[0]
    earlier = (ranking[None, :] < ranking[:, None]).astype(jnp.float32)
    expert_range = lax.broadcasted_iota(jnp.int32, (1, 1, buckets), 2)
    matches = (expert_ids[:, :, None] == expert_range).astype(jnp.float32)
    routed = jnp.sum(matches, axis=1)
    before = jnp.dot(earlier, routed)
    slot_rank = jnp.sum(matches * before[:, None, :], axis=2)
    keep_limit = jnp.sum(matches * cap_counts.astype(jnp.float32)[None, None, :], axis=2)
    slot_range = lax.broadcasted_iota(jnp.float32, (1, 1, capacity), 2)
    slot_hit = (
        (slot_rank[:, :, None] == slot_range) & (slot_rank < keep_limit)[:, :, None]
    ).astype(jnp.float32)
    placement = matches[:, :, :, None] * slot_hit[:, :, None, :]
    return placement.reshape(expert_ids.shape[0], expert_ids.shape[1], buckets * capacity)


def expert_core(slot_x, slot_q, slot_scale, slot_prob, w_gate, w_up, w_down):
    gate_pre = contract_last(slot_x, w_gate)
    up_pre = contract_last(slot_x, w_up)
    back_proj = contract_last(slot_q, w_down)
    squash = jax.nn.sigmoid(sharpness * gate_pre)
    gated = gate_pre * squash
    activated = (up_pre + 1.0) * gated
    weight = (slot_scale * slot_prob)[:, None]
    act_delta = weight * back_proj
    up_delta = (act_delta * gated).astype(jnp.bfloat16)
    gate_delta = (
        act_delta * (up_pre + 1.0) * (squash + sharpness * gate_pre * squash * (1.0 - squash))
    ).astype(jnp.bfloat16)
    act_scaled = (activated * weight).astype(jnp.bfloat16)
    in_delta = jnp.dot(gate_delta, w_gate, preferred_element_type=jnp.float32) + jnp.dot(
        up_delta, w_up, preferred_element_type=jnp.float32
    )
    return (activated, back_proj, gate_delta, up_delta, act_scaled, in_delta)


def returned_term(activated, back_proj, slot_scale):
    return slot_scale * jnp.sum(activated * back_proj, axis=1)


def on_device(
    grad_out, tokens, probs, expert_ids, priority, cap_counts, gate_weight, up_weight, down_weight
):
    ep_size = lax.axis_size("ep")
    tok_rows, model_width = tokens.shape
    route_count = expert_ids.shape[1]
    capacity = 5 * route_count * tok_rows // (4 * ep_size)
    slot_rows = ep_size * capacity
    placement = route_table(expert_ids, priority, cap_counts, ep_size, capacity)
    slot_table = jnp.sum(placement, axis=1)
    table_low = slot_table.astype(jnp.bfloat16)
    row_scale = jnp.maximum(jnp.max(jnp.abs(grad_out), axis=1), 1.0)
    quantized = (grad_out / row_scale[:, None]).astype(jnp.bfloat16)
    send_x = jnp.einsum("ts,td->sd", table_low, tokens, preferred_element_type=jnp.float32).astype(
        jnp.bfloat16
    )
    send_q = jnp.einsum(
        "ts,td->sd", table_low, quantized, preferred_element_type=jnp.float32
    ).astype(jnp.bfloat16)
    send_scale = jnp.sum(slot_table * row_scale[:, None], axis=0)
    send_prob = jnp.sum(placement * probs[:, :, None], axis=(0, 1))
    bucket_shape = (ep_size, capacity, model_width)
    recv_x, recv_q, recv_scale, recv_prob = (
        lax.all_to_all(send_x.reshape(bucket_shape), "ep", split_axis=0, concat_axis=0, tiled=True),
        lax.all_to_all(send_q.reshape(bucket_shape), "ep", split_axis=0, concat_axis=0, tiled=True),
        lax.all_to_all(
            send_scale.reshape(ep_size, capacity).astype(jnp.bfloat16),
            "ep",
            split_axis=0,
            concat_axis=0,
            tiled=True,
        ).astype(jnp.float32),
        lax.all_to_all(
            send_prob.reshape(ep_size, capacity).astype(jnp.bfloat16),
            "ep",
            split_axis=0,
            concat_axis=0,
            tiled=True,
        ).astype(jnp.float32),
    )
    slot_x = recv_x.reshape(slot_rows, model_width)
    slot_q = recv_q.reshape(slot_rows, model_width)
    slot_scale = recv_scale.reshape(slot_rows)
    slot_prob = recv_prob.reshape(slot_rows)
    w_gate = gate_weight[0]
    w_up = up_weight[0]
    w_down = down_weight[0]
    activated, back_proj, gate_delta, up_delta, act_scaled, in_delta = expert_core(
        slot_x, slot_q, slot_scale, slot_prob, w_gate, w_up, w_down
    )
    slot_in = in_delta.astype(jnp.bfloat16)
    slot_out = returned_term(activated, back_proj, slot_scale)
    summed = lax.psum_scatter(
        jnp.concatenate(
            [
                contract_first(gate_delta, slot_x),
                contract_first(up_delta, slot_x),
                contract_first(act_scaled, slot_q),
            ],
            axis=1,
        ).astype(jnp.bfloat16),
        "dp",
        scatter_dimension=0,
        tiled=True,
    ).astype(jnp.float32)
    gate_share = summed[:, :model_width].astype(jnp.bfloat16)
    up_share = summed[:, model_width : 2 * model_width].astype(jnp.bfloat16)
    down_share = summed[:, 2 * model_width :].astype(jnp.bfloat16)
    back_in, back_prob = (
        lax.all_to_all(
            slot_in.reshape(bucket_shape), "ep", split_axis=0, concat_axis=0, tiled=True
        ),
        lax.all_to_all(
            shortened(slot_out.reshape(ep_size, capacity)),
            "ep",
            split_axis=0,
            concat_axis=0,
            tiled=True,
        ),
    )
    prob_grad = jnp.einsum("tks,s->tk", placement, back_prob.reshape(slot_rows))
    input_grad = jnp.einsum(
        "ts,sd->td",
        table_low,
        back_in.reshape(slot_rows, model_width),
        preferred_element_type=jnp.float32,
    ).astype(jnp.bfloat16)
    return (input_grad, prob_grad, gate_share[None], up_share[None], down_share[None])


def solution(mesh):
    return jax.shard_map(
        on_device,
        mesh=mesh,
        in_specs=(
            P(("ep", "dp"), None),
            P(("ep", "dp"), None),
            P(("ep", "dp"), None),
            P(("ep", "dp"), None),
            P(("ep", "dp"), None),
            P(),
            P("ep", None, None),
            P("ep", None, None),
            P("ep", None, None),
        ),
        out_specs=(
            P(("ep", "dp"), None),
            P(("ep", "dp"), None),
            P("ep", "dp", None),
            P("ep", "dp", None),
            P("ep", "dp", None),
        ),
        check_vma=False,
    )
```

profile of v0, /device:TPU:1, one launch (start us, length us, event | category | flops | bytes accessed | tf_op | source)
XLA Modules:
  0.0 330.3 jit_solution(7792389027727530450)
XLA Ops:
  12.7 9.4 %all-to-all-start.1 = ((bf16[32,1,20]{2,1,0:T(2,128)(2,1)}), bf16[32,1,20]{2,1,0:T(2,128)(2,1)S(1)}, u32[]{:S(2)}, u32[]{:S(2)}) async-start(bf16[32,1,20]{2,1,0:T(2,128)(2,1)} %copy.80), calls=%async_computation.1 | async-start | bytes 32768 | tf_op jit(solution)/shard_map/all_to_all | solution.py:102
  24.4 4.6 %all-to-all-done.1 = bf16[32,1,20]{2,1,0:T(2,128)(2,1)S(1)} async-done(((bf16[32,1,20]{2,1,0:T(2,128)(2,1)}), bf16[32,1,20]{2,1,0:T(2,128)(2,1)S(1)}, u32[]{:S(2)}, u32[]{:S(2)}) %all-to-all-start.1) | async-done | bytes 1312 | tf_op jit(solution)/shard_map/all_to_all | solution.py:102
  29.0 4.1 %all-to-all-start = ((bf16[32,1,20]{2,1,0:T(2,128)(2,1)}), bf16[32,1,20]{2,1,0:T(2,128)(2,1)S(1)}, u32[]{:S(2)}, u32[]{:S(2)}) async-start(bf16[32,1,20]{2,1,0:T(2,128)(2,1)} %copy.78), calls=%async_computation | async-start | bytes 32768 | tf_op jit(solution)/shard_map/all_to_all | solution.py:95
  33.8 2.1 reshape.113
  35.9 4.2 %all-to-all-done = bf16[32,1,20]{2,1,0:T(2,128)(2,1)S(1)} async-done(((bf16[32,1,20]{2,1,0:T(2,128)(2,1)}), bf16[32,1,20]{2,1,0:T(2,128)(2,1)S(1)}, u32[]{:S(2)}, u32[]{:S(2)}) %all-to-all-start) | async-done | bytes 1312 | tf_op jit(solution)/shard_map/all_to_all | solution.py:95
  40.2 4.4 %all-to-all-start.3 = ((bf16[32,20,1536]{2,1,0:T(8,128)(2,1)}), bf16[32,20,1536]{2,1,0:T(8,128)(2,1)S(1)}, u32[]{:S(2)}, u32[]{:S(2)}) async-start(bf16[32,20,1536]{2,1,0:T(8,128)(2,1)} %reshape.113), calls=%async_computation.3 | async-start | bytes 4718592 | tf_op jit(solution)/shard_map/all_to_all | solution.py:93
  44.5 3.2 convolution_convert_fusion.4
  47.7 4.0 %reshape.111 = bf16[32,20,1536]{2,1,0:T(8,128)(2,1)} reshape(bf16[640,1536]{1,0:T(8,128)(2,1)} %convolution_convert_fusion.4) | data formatting | bytes 3932160 | tf_op jit(solution)/shard_map/reshape | solution.py:94
  51.7 24.1 %all-to-all-done.3 = bf16[32,20,1536]{2,1,0:T(8,128)(2,1)S(1)} async-done(((bf16[32,20,1536]{2,1,0:T(8,128)(2,1)}), bf16[32,20,1536]{2,1,0:T(8,128)(2,1)S(1)}, u32[]{:S(2)}, u32[]{:S(2)}) %all-to-all-start.3) | async-done | bytes 1966112 | tf_op jit(solution)/shard_map/all_to_all | solution.py:93
  75.8 6.7 %all-to-all-start.2 = ((bf16[32,20,1536]{2,1,0:T(8,128)(2,1)}), bf16[32,20,1536]{2,1,0:T(8,128)(2,1)}, u32[]{:S(2)}, u32[]{:S(2)}) async-start(bf16[32,20,1536]{2,1,0:T(8,128)(2,1)} %reshape.111), calls=%async_computation.2 | async-start | bytes 4718592 | tf_op jit(solution)/shard_map/all_to_all | solution.py:94
  82.6 2.0 reshape.114
  84.6 8.2 %fusion.2 = f32[640,1536]{1,0:T(8,128)} fusion(bf16[640,1536]{1,0:T(8,128)(2,1)} %reshape.114, bf16[1,1536,1536]{2,1,0:T(8,128)(2,1)} %param.15), kind=kOutput, calls=%fused_computation.6 | convolution fusion | flops 3019898880 | bytes 10616832 | tf_op jit(solution)/shard_map/dot_general | solution.py:18
  92.8 7.5 %fusion.6 = f32[640,1536]{1,0:T(8,128)} fusion(bf16[640,1536]{1,0:T(8,128)(2,1)S(1)} %copy-done.2, bf16[1,1536,1536]{2,1,0:T(8,128)(2,1)} %param.16), kind=kOutput, calls=%fused_computation.10 | convolution fusion | flops 3019898880 | bytes 10616832 | tf_op jit(solution)/shard_map/dot_general | solution.py:18
  100.3 13.5 %all-to-all-done.2 = bf16[32,20,1536]{2,1,0:T(8,128)(2,1)} async-done(((bf16[32,20,1536]{2,1,0:T(8,128)(2,1)}), bf16[32,20,1536]{2,1,0:T(8,128)(2,1)}, u32[]{:S(2)}, u32[]{:S(2)}) %all-to-all-start.2) | async-done | bytes 1966112 | tf_op jit(solution)/shard_map/all_to_all | solution.py:94
  113.8 4.0 %reshape.112 = bf16[640,1536]{1,0:T(8,128)(2,1)} reshape(bf16[32,20,1536]{2,1,0:T(8,128)(2,1)} %all-to-all-done.2) | data formatting | bytes 3932160 | tf_op jit(solution)/shard_map/reshape | solution.py:111
  117.7 8.4 %convolution_convert_fusion = bf16[1536,1536]{0,1:T(8,128)(2,1)S(1)} fusion(bf16[640,1536]{1,0:T(8,128)(2,1)} %reshape.112, f32[640]{0:T(1024)S(1)} %mul.119, f32[640,1536]{1,0:T(8,128)} %fusion.6, f32[640,1536]{1,0:T(8,128)} %fusion.2), kind=kOutput, calls=%fused_computation.1 | convolution fusion | flops 3031105536 | bytes 14551552 | tf_op jit(solution)/shard_map/dot_general | solution.py:24
  126.1 6.9 %multiply_reduce_fusion = (f32[640]{0:T(1024)S(1)}, bf16[640,1536]{1,0:T(8,128)(2,1)S(1)}, bf16[640,1536]{1,0:T(8,128)(2,1)S(1)}) fusion(f32[640,1536]{1,0:T(8,128)S(1)} %copy-done.5, f32[640,1536]{1,0:T(8,128)S(1)} %copy-done.4, f32[640]{0:T(1024)S(1)} %mul.119, bf16[640,1536]{1,0:T(8,128)(2,1)S(1)} %copy-done.3, bf16[1,1536,1536]{2,1,0:T(8,128)(2,1)} %param.17), kind=kOutput, calls=%fused_computation.15 | convolution fusion | flops 3038576128 | bytes 18486272 | tf_op jit(solution)/shard_map/dot_general | solution.py:18
  133.1 4.2 %convolution_convert_fusion.1 = bf16[1536,1536]{0,1:T(8,128)(2,1)S(1)} fusion(bf16[640,1536]{1,0:T(8,128)(2,1)S(1)} %get-tuple-element.46, bf16[640,1536]{1,0:T(8,128)(2,1)S(1)} %copy-done.2), kind=kOutput, calls=%fused_computation.2 | convolution fusion | flops 3022258176 | bytes 8650752 | tf_op jit(solution)/shard_map/dot_general | solution.py:24
  137.3 4.2 %convolution_convert_fusion.2 = bf16[1536,1536]{0,1:T(8,128)(2,1)S(1)} fusion(bf16[640,1536]{1,0:T(8,128)(2,1)S(1)} %get-tuple-element.45, bf16[640,1536]{1,0:T(8,128)(2,1)S(1)} %copy-done.2), kind=kOutput, calls=%fused_computation.3 | convolution fusion | flops 3022258176 | bytes 8650752 | tf_op jit(solution)/shard_map/dot_general | solution.py:24
  141.5 24.3 %pad_maximum_fusion = bf16[1536,4608]{0,1:T(8,128)(2,1)} fusion(bf16[1536,1536]{0,1:T(8,128)(2,1)S(1)} %convolution_convert_fusion, bf16[1536,1536]{0,1:T(8,128)(2,1)S(1)} %convolution_convert_fusion.1, bf16[1536,1536]{0,1:T(8,128)(2,1)S(1)} %convolution_convert_fusion.2), kind=kLoop, calls=%fused_computation | loop fusion | flops 42467328 | bytes 28311552 | tf_op jit(solution)/shard_map/concatenate | solution.py:123
  165.8 17.8 %copy.91 = bf16[1536,4608]{1,0:T(8,128)(2,1)} copy(bf16[1536,4608]{0,1:T(8,128)(2,1)} %pad_maximum_fusion) | data formatting | bytes 28311552
  184.3 5.7 %all-to-all-start.5 = ((bf16[32,1,20]{2,1,0:T(2,128)(2,1)}), bf16[32,1,20]{2,1,0:T(2,128)(2,1)S(1)}, u32[]{:S(2)}, u32[]{:S(2)}) async-start(bf16[32,1,20]{2,1,0:T(2,128)(2,1)} %copy.84), calls=%async_computation.5 | async-start | bytes 32768 | tf_op jit(solution)/shard_map/all_to_all | solution.py:142
  190.1 5.9 %fusion = f32[640,1536]{1,0:T(8,128)S(1)} fusion(bf16[640,1536]{1,0:T(8,128)(2,1)S(1)} %copy-done.9, bf16[1,1536,1536]{2,1,0:T(8,128)(2,1)} %param.15), kind=kOutput, calls=%fused_computation.4 | convolution fusion | flops 3019898880 | bytes 10616832 | tf_op jit(solution)/shard_map/dot_general | solution.py:60
  196.0 5.5 %add_convert_fusion = bf16[640,1536]{1,0:T(8,128)(2,1)S(1)} fusion(f32[640,1536]{1,0:T(8,128)S(1)} %fusion, bf16[640,1536]{1,0:T(8,128)(2,1)S(1)} %copy-done.7, bf16[1,1536,1536]{2,1,0:T(8,128)(2,1)} %param.16), kind=kOutput, calls=%fused_computation.16 | convolution fusion | flops 3021864960 | bytes 12582912 | tf_op jit(solution)/shard_map/dot_general | solution.py:60
  201.5 2.1 reshape.115
  203.6 7.5 %all-to-all-start.4 = ((bf16[32,20,1536]{2,1,0:T(8,128)(2,1)}), bf16[32,20,1536]{2,1,0:T(8,128)(2,1)S(1)}, u32[]{:S(2)}, u32[]{:S(2)}) async-start(bf16[32,20,1536]{2,1,0:T(8,128)(2,1)} %reshape.115), calls=%async_computation.4 | async-start | bytes 4718592 | tf_op jit(solution)/shard_map/all_to_all | solution.py:139
  212.0 30.6 %all-to-all-done.4 = bf16[32,20,1536]{2,1,0:T(8,128)(2,1)S(1)} async-done(((bf16[32,20,1536]{2,1,0:T(8,128)(2,1)}), bf16[32,20,1536]{2,1,0:T(8,128)(2,1)S(1)}, u32[]{:S(2)}, u32[]{:S(2)}) %all-to-all-start.4) | async-done | bytes 1966112 | tf_op jit(solution)/shard_map/all_to_all | solution.py:139
  244.1 65.4 %reduce-scatter.4.cloned.1.call-done = bf16[384,4608]{1,0:T(8,128)(2,1)} async-done(((bf16[1536,4608]{1,0:T(8,128)(2,1)}), bf16[384,4608]{1,0:T(8,128)(2,1)}) %reduce-scatter.4.cloned.1.call-update) | async-done | bytes 3538960
  309.6 3.2 fusion.34
  312.8 2.4 copy.96
  315.2 2.4 copy.88
  318.9 2.4 copy.87
  (50 shorter events, 15.4 us)
Async XLA Ops:
  7.2 26.0 %copy-start = (bf16[128,1536]{1,0:T(8,128)(2,1)S(1)}, bf16[128,1536]{1,0:T(8,128)(2,1)}, u32[]{:S(2)}) copy-start(bf16[128,1536]{1,0:T(8,128)(2,1)} %param.10) | copy-start | bytes 1179652
  12.7 16.3 %all-to-all-start.1 = ((bf16[32,1,20]{2,1,0:T(2,128)(2,1)}), bf16[32,1,20]{2,1,0:T(2,128)(2,1)S(1)}, u32[]{:S(2)}, u32[]{:S(2)}) async-start(bf16[32,1,20]{2,1,0:T(2,128)(2,1)} %copy.80), calls=%async_computation.1 | async-start | bytes 32768 | tf_op jit(solution)/shard_map/all_to_all | solution.py:102
  29.0 11.1 %all-to-all-start = ((bf16[32,1,20]{2,1,0:T(2,128)(2,1)}), bf16[32,1,20]{2,1,0:T(2,128)(2,1)S(1)}, u32[]{:S(2)}, u32[]{:S(2)}) async-start(bf16[32,1,20]{2,1,0:T(2,128)(2,1)} %copy.78), calls=%async_computation | async-start | bytes 32768 | tf_op jit(solution)/shard_map/all_to_all | solution.py:95
  40.2 35.6 %all-to-all-start.3 = ((bf16[32,20,1536]{2,1,0:T(8,128)(2,1)}), bf16[32,20,1536]{2,1,0:T(8,128)(2,1)S(1)}, u32[]{:S(2)}, u32[]{:S(2)}) async-start(bf16[32,20,1536]{2,1,0:T(8,128)(2,1)} %reshape.113), calls=%async_computation.3 | async-start | bytes 4718592 | tf_op jit(solution)/shard_map/all_to_all | solution.py:93
  75.8 38.0 %all-to-all-start.2 = ((bf16[32,20,1536]{2,1,0:T(8,128)(2,1)}), bf16[32,20,1536]{2,1,0:T(8,128)(2,1)}, u32[]{:S(2)}, u32[]{:S(2)}) async-start(bf16[32,20,1536]{2,1,0:T(8,128)(2,1)} %reshape.111), calls=%async_computation.2 | async-start | bytes 4718592 | tf_op jit(solution)/shard_map/all_to_all | solution.py:94
  82.5 227.1 %reduce-scatter.4.cloned.1.call-start = ((), (), s32[]{:S(2)}) async-start(), calls=%async_computation.7 | async-start | bytes 17694720
  84.6 8.2 %copy-start.2 = (bf16[640,1536]{1,0:T(8,128)(2,1)S(1)}, bf16[640,1536]{1,0:T(8,128)(2,1)}, u32[]{:S(2)}) copy-start(bf16[640,1536]{1,0:T(8,128)(2,1)} %reshape.114) | copy-start | bytes 5898244
  117.7 8.4 %copy-start.3 = (bf16[640,1536]{1,0:T(8,128)(2,1)S(1)}, bf16[640,1536]{1,0:T(8,128)(2,1)}, u32[]{:S(2)}) copy-start(bf16[640,1536]{1,0:T(8,128)(2,1)} %reshape.112) | copy-start | bytes 5898244
  117.7 8.4 %copy-start.4 = (f32[640,1536]{1,0:T(8,128)S(1)}, f32[640,1536]{1,0:T(8,128)}, u32[]{:S(2)}) copy-start(f32[640,1536]{1,0:T(8,128)} %fusion.2) | copy-start | bytes 11796484
  117.7 8.4 %copy-start.5 = (f32[640,1536]{1,0:T(8,128)S(1)}, f32[640,1536]{1,0:T(8,128)}, u32[]{:S(2)}) copy-start(f32[640,1536]{1,0:T(8,128)} %fusion.6) | copy-start | bytes 11796484
  133.1 4.2 %copy-start.6 = (bf16[640,1536]{1,0:T(8,128)(2,1)}, bf16[640,1536]{1,0:T(8,128)(2,1)S(1)}, u32[]{:S(2)}) copy-start(bf16[640,1536]{1,0:T(8,128)(2,1)S(1)} %get-tuple-element.46) | copy-start | bytes 5898244
  133.1 4.2 %copy-start.8 = (bf16[640,1536]{1,0:T(8,128)(2,1)}, bf16[640,1536]{1,0:T(8,128)(2,1)S(1)}, u32[]{:S(2)}) copy-start(bf16[640,1536]{1,0:T(8,128)(2,1)S(1)} %get-tuple-element.45) | copy-start | bytes 5898244
  183.6 6.5 %copy-start.9 = (bf16[640,1536]{1,0:T(8,128)(2,1)S(1)}, bf16[640,1536]{1,0:T(8,128)(2,1)}, u32[]{:S(2)}) copy-start(bf16[640,1536]{1,0:T(8,128)(2,1)} %copy-done.8) | copy-start | bytes 5898244
  184.3 19.3 %all-to-all-start.5 = ((bf16[32,1,20]{2,1,0:T(2,128)(2,1)}), bf16[32,1,20]{2,1,0:T(2,128)(2,1)S(1)}, u32[]{:S(2)}, u32[]{:S(2)}) async-start(bf16[32,1,20]{2,1,0:T(2,128)(2,1)} %copy.84), calls=%async_computation.5 | async-start | bytes 32768 | tf_op jit(solution)/shard_map/all_to_all | solution.py:142
  190.1 5.9 %copy-start.7 = (bf16[640,1536]{1,0:T(8,128)(2,1)S(1)}, bf16[640,1536]{1,0:T(8,128)(2,1)}, u32[]{:S(2)}) copy-start(bf16[640,1536]{1,0:T(8,128)(2,1)} %copy-done.6) | copy-start | bytes 5898244
  203.6 39.0 %all-to-all-start.4 = ((bf16[32,20,1536]{2,1,0:T(8,128)(2,1)}), bf16[32,20,1536]{2,1,0:T(8,128)(2,1)S(1)}, u32[]{:S(2)}, u32[]{:S(2)}) async-start(bf16[32,20,1536]{2,1,0:T(8,128)(2,1)} %reshape.115), calls=%async_computation.4 | async-start | bytes 4718592 | tf_op jit(solution)/shard_map/all_to_all | solution.py:139
  317.5 6.0 %copy-start.1 = (bf16[128,1536]{1,0:T(8,128)(2,1)S(1)}, bf16[128,1536]{1,0:T(8,128)(2,1)}, u32[]{:S(2)}) copy-start(bf16[128,1536]{1,0:T(8,128)(2,1)} %param.10) | copy-start | bytes 1179652
Sparse Core Ops, SparseCore 0:
  183.7 125.8 reduce-scatter.3
where the time goes:
time: 332 us; the launch traced here: 330 us
  waiting for transfers between devices  142 us (43%)
  matrix products  57.8 us (17%)
  local copies, waits for them, and re-layouts  48.3 us (15%)
  starting transfers between devices  37.8 us (11%)
  other arithmetic  29.6 us (9%)
  between operations  14.3 us (4%)
    unnamed x2, waiting for transfers between devices  65.4 us
    all_to_all x1, waiting for transfers between devices, on_device(): lax.all_to_all(slot_in.reshape(bucket_shape), 'ep', split_axis=0, concat_...  30.6 us
    unnamed x27, local copies, waits for them, and re-layouts  28.5 us
    concatenate x1, other arithmetic, on_device(): jnp.concatenate([contract_first(gate_delta, slot_x), contract_first(up_de...  24.3 us
    all_to_all x1, waiting for transfers between devices, on_device(): lax.all_to_all(send_x.reshape(bucket_shape), 'ep', split_axis=0, concat_a...  24.1 us
    dot_general x3, matrix products, contract_last(): lax.dot_general(first_op, second_op, (((1,), (1,)), ((), ())), preferred_...  22.6 us
    dot_general x3, matrix products, contract_first(): lax.dot_general(first_op, second_op, (((0,), (0,)), ((), ())), preferred_...  16.7 us
    all_to_all x1, waiting for transfers between devices, on_device(): lax.all_to_all(send_q.reshape(bucket_shape), 'ep', split_axis=0, concat_a...  13.5 us
  transfers between devices with their start and end apart: 7, of which 6 were waited for; matrix products, arithmetic and copies ran while one was open for 14% of the time, Pallas kernels for 0%

commit v1 on v0

v1 whole, which is shorter than its diff:
```python
import jax
import jax.numpy as jnp
from jax import lax
from jax.sharding import PartitionSpec as P

sharpness = 1.702


def contract_last(first_op, second_op):
    return lax.dot_general(
        first_op, second_op, (((1,), (1,)), ((), ())), preferred_element_type=jnp.float32
    )


def contract_first(first_op, second_op):
    return lax.dot_general(
        first_op, second_op, (((0,), (0,)), ((), ())), preferred_element_type=jnp.float32
    )


def route_table(expert_ids, priority, cap_counts, buckets, capacity):
    ranking = priority[0]
    earlier = (ranking[None, :] < ranking[:, None]).astype(jnp.float32)
    expert_range = lax.broadcasted_iota(jnp.int32, (1, 1, buckets), 2)
    matches = (expert_ids[:, :, None] == expert_range).astype(jnp.float32)
    routed = jnp.sum(matches, axis=1)
    before = jnp.dot(earlier, routed)
    slot_rank = jnp.sum(matches * before[:, None, :], axis=2)
    keep_limit = jnp.sum(matches * cap_counts.astype(jnp.float32)[None, None, :], axis=2)
    slot_range = lax.broadcasted_iota(jnp.float32, (1, 1, capacity), 2)
    slot_hit = (
        (slot_rank[:, :, None] == slot_range) & (slot_rank < keep_limit)[:, :, None]
    ).astype(jnp.float32)
    placement = matches[:, :, :, None] * slot_hit[:, :, None, :]
    return placement.reshape(expert_ids.shape[0], expert_ids.shape[1], buckets * capacity)


def deltas(slot_x, slot_g, w_gate, w_up, w_down):
    gate_pre = contract_last(slot_x, w_gate)
    up_pre = contract_last(slot_x, w_up)
    act_delta = contract_last(slot_g, w_down)
    squash = jax.nn.sigmoid(sharpness * gate_pre)
    gated = gate_pre * squash
    activated = (up_pre + 1.0) * gated
    up_delta = (act_delta * gated).astype(jnp.bfloat16)
    gate_delta = (
        act_delta * (up_pre + 1.0) * (squash + sharpness * gate_pre * squash * (1.0 - squash))
    ).astype(jnp.bfloat16)
    return activated, act_delta, gate_delta, up_delta


def on_device(
    grad_out, tokens, probs, expert_ids, priority, cap_counts, gate_weight, up_weight, down_weight
):
    ep_size = lax.axis_size("ep")
    dp_size = lax.axis_size("dp")
    tok_rows, model_width = tokens.shape
    route_count = expert_ids.shape[1]
    capacity = 5 * route_count * tok_rows // (4 * ep_size)
    slot_rows = ep_size * capacity
    placement = route_table(expert_ids, priority, cap_counts, ep_size, capacity)
    slot_table = jnp.sum(placement, axis=1)
    table_low = slot_table.astype(jnp.bfloat16)
    row_scale = jnp.maximum(jnp.max(jnp.abs(grad_out), axis=1), 1.0)
    quantized = (grad_out / row_scale[:, None]).astype(jnp.bfloat16)
    send_prob = jnp.sum(placement * probs[:, :, None], axis=(0, 1))
    send_scale = jnp.sum(slot_table * row_scale[:, None], axis=0)
    send_x = jnp.einsum("ts,td->sd", table_low, tokens, preferred_element_type=jnp.float32).astype(
        jnp.bfloat16
    )
    send_g = (
        jnp.einsum("ts,td->sd", table_low, quantized, preferred_element_type=jnp.float32)
        * (send_prob * send_scale)[:, None]
    ).astype(jnp.bfloat16)
    bucket_shape = (ep_size, capacity, model_width)

    def exchange(a):
        return lax.all_to_all(a, "ep", split_axis=0, concat_axis=0, tiled=True)

    slot_x = exchange(send_x.reshape(bucket_shape)).reshape(slot_rows, model_width)
    all_x = lax.all_gather(slot_x, "dp", axis=0, tiled=True)
    slot_g = exchange(send_g.reshape(bucket_shape)).reshape(slot_rows, model_width)
    all_g = lax.all_gather(slot_g, "dp", axis=0, tiled=True)
    w_gate = gate_weight[0]
    w_up = up_weight[0]
    w_down = down_weight[0]
    activated, act_delta, gate_delta, up_delta = deltas(slot_x, slot_g, w_gate, w_up, w_down)
    slot_in = (
        jnp.dot(gate_delta, w_gate, preferred_element_type=jnp.float32)
        + jnp.dot(up_delta, w_up, preferred_element_type=jnp.float32)
    ).astype(jnp.bfloat16)
    slot_out = jnp.sum(activated * act_delta, axis=1)
    back_in = exchange(slot_in.reshape(bucket_shape))
    back_prob = exchange(slot_out.reshape(ep_size, capacity).astype(jnp.bfloat16))
    prob_grad = jnp.einsum("tks,s->tk", placement, back_prob.reshape(slot_rows)) / probs
    input_grad = jnp.einsum(
        "ts,sd->td",
        table_low,
        back_in.reshape(slot_rows, model_width),
        preferred_element_type=jnp.float32,
    ).astype(jnp.bfloat16)
    share = w_gate.shape[0] // dp_size
    first = lax.axis_index("dp") * share

    def mine(w):
        return lax.dynamic_slice_in_dim(w, first, share, 0)

    act_mine, _, gd_mine, ud_mine = deltas(all_x, all_g, mine(w_gate), mine(w_up), mine(w_down))
    gate_share = contract_first(gd_mine, all_x).astype(jnp.bfloat16)
    up_share = contract_first(ud_mine, all_x).astype(jnp.bfloat16)
    down_share = contract_first(act_mine.astype(jnp.bfloat16), all_g).astype(jnp.bfloat16)
    return (input_grad, prob_grad, gate_share[None], up_share[None], down_share[None])


def solution(mesh):
    return jax.shard_map(
        on_device,
        mesh=mesh,
        in_specs=(
            P(("ep", "dp"), None),
            P(("ep", "dp"), None),
            P(("ep", "dp"), None),
            P(("ep", "dp"), None),
            P(("ep", "dp"), None),
            P(),
            P("ep", None, None),
            P("ep", None, None),
            P("ep", None, None),
        ),
        out_specs=(
            P(("ep", "dp"), None),
            P(("ep", "dp"), None),
            P("ep", "dp", None),
            P("ep", "dp", None),
            P("ep", "dp", None),
        ),
        check_vma=False,
    )
```

time: 332 us -> 249 us (0.75)
  waiting for transfers between devices: 142 us -> 47.5 us
  blocking collectives: 0 us -> 75.7 us
  local copies, waits for them, and re-layouts: 48.3 us -> 16.4 us
  starting transfers between devices: 37.8 us -> 11.2 us
  other arithmetic: 29.6 us -> 5.9 us
  matrix products: 57.8 us -> 76.9 us
    all_to_all x0 -> x2, blocking collectives: none -> 75.7 us  [exchange(): return lax.all_to_all(a, 'ep', split_axis=0, concat_axis=0, tiled=True)]
    unnamed x2, waiting for transfers between devices: 65.4 us -> 0.03 us
    all_to_all x6 -> x2, waiting for transfers between devices: 77 us -> 30.6 us  [exchange(): return lax.all_to_all(a, 'ep', split_axis=0, concat_axis=0, tiled=True)]
    unnamed x27 -> x36, local copies, waits for them, and re-layouts: 28.5 us -> 0.09 us
    all_to_all x6 -> x2, starting transfers between devices: 37.8 us -> 11.1 us  [exchange(): return lax.all_to_all(a, 'ep', split_axis=0, concat_axis=0, tiled=True)]
    concatenate x1 -> x0, other arithmetic: 24.3 us -> none  [on_device(): jnp.concatenate([contract_first(gate_delta, slot_x), contract_first(up_de...]
    dot_general x3 -> x6, matrix products: 22.6 us -> 42 us  [contract_last(): lax.dot_general(first_op, second_op, (((1,), (1,)), ((), ())), preferred_...]
    all_gather x0 -> x2, waiting for transfers between devices: none -> 16.9 us  [the longest x1 16.9 us: on_device(): all_g = lax.all_gather(slot_g, 'dp', axis=0, tiled=True)]
  transfers between devices with their start and end apart: 7 -> 4, of which waited for: 6 -> 2; matrix products, arithmetic and copies ran while one was open for 14% -> 26% of each run, Pallas kernels for 0% -> 0%
where the time goes in v1:
time: 249 us; the launch traced here: 248 us
  matrix products  76.9 us (31%)
  blocking collectives  75.7 us (30%)
  waiting for transfers between devices  47.5 us (19%)
  local copies, waits for them, and re-layouts  16.4 us (7%)
  between operations  14.4 us (6%)
  starting transfers between devices  11.2 us (4%)
  other arithmetic  5.9 us (2%)
    all_to_all x2, blocking collectives, exchange(): return lax.all_to_all(a, 'ep', split_axis=0, concat_axis=0, tiled=True)  75.7 us
    dot_general x6, matrix products, contract_last(): lax.dot_general(first_op, second_op, (((1,), (1,)), ((), ())), preferred_...  42 us
    all_to_all x2, waiting for transfers between devices, exchange(): return lax.all_to_all(a, 'ep', split_axis=0, concat_axis=0, tiled=True)  30.6 us
    all_gather x1, waiting for transfers between devices, on_device(): all_g = lax.all_gather(slot_g, 'dp', axis=0, tiled=True)  16.9 us
    dot_general x3, matrix products, contract_first(): lax.dot_general(first_op, second_op, (((0,), (0,)), ((), ())), preferred_...  13.4 us
    all_to_all x2, starting transfers between devices, exchange(): return lax.all_to_all(a, 'ep', split_axis=0, concat_axis=0, tiled=True)  11.1 us
    dot_general x1, matrix products, on_device(): jnp.dot(gate_delta, w_gate, preferred_element_type=jnp.float32)  8.95 us
    dot_general x1, matrix products, on_device(): jnp.dot(up_delta, w_up, preferred_element_type=jnp.float32)  5.8 us
  transfers between devices with their start and end apart: 4, of which 2 were waited for; matrix products, arithmetic and copies ran while one was open for 26% of the time, Pallas kernels for 0%

profile of v1, /device:TPU:1, one launch (start us, length us, event | category | flops | bytes accessed | tf_op | source)
XLA Modules:
  0.0 248.0 jit_solution(7221112332950681031)
XLA Ops:
  7.2 0.7 convert_element_type.78
  8.6 0.8 select_reduce_fusion
  9.4 0.9 fusion.40
  10.3 0.7 select_reduce_fusion.1
  11.1 1.3 abs_reduce_fusion
  12.4 1.0 fusion.24
  13.6 1.9 convolution_convert_fusion
  15.6 2.5 reshape.94
  18.0 40.7 %all_to_all.24 = bf16[32,20,1536]{2,1,0:T(8,128)(2,1)} all-to-all(bf16[32,20,1536]{2,1,0:T(8,128)(2,1)S(1)} %reshape.94), channel_id=1, replica_groups=mesh['ep'=32,'dp'=4] {'ep'}, dimensions={0} | all-to-all | bytes 3932160 | tf_op jit(solution)/shard_map/all_to_all | solution.py:78
  58.7 4.1 %reshape.95 = bf16[640,1536]{1,0:T(8,128)(2,1)} reshape(bf16[32,20,1536]{2,1,0:T(8,128)(2,1)} %all_to_all.24) | data formatting | bytes 3932160 | tf_op jit(solution)/shard_map/reshape | solution.py:80
  63.1 2.1 multiply_convert_fusion.5
  65.2 2.5 reshape.92
  67.6 35.0 %all_to_all.25 = bf16[32,20,1536]{2,1,0:T(8,128)(2,1)} all-to-all(bf16[32,20,1536]{2,1,0:T(8,128)(2,1)S(1)} %reshape.92), channel_id=1, replica_groups=mesh['ep'=32,'dp'=4] {'ep'}, dimensions={0} | all-to-all | bytes 3932160 | tf_op jit(solution)/shard_map/all_to_all | solution.py:78
  102.6 4.1 %reshape.93 = bf16[640,1536]{1,0:T(8,128)(2,1)} reshape(bf16[32,20,1536]{2,1,0:T(8,128)(2,1)} %all_to_all.25) | data formatting | bytes 3932160 | tf_op jit(solution)/shard_map/reshape | solution.py:82
  106.8 5.3 %fusion.6 = f32[640,1536]{1,0:T(8,128)S(1)} fusion(bf16[640,1536]{1,0:T(8,128)(2,1)S(1)} %copy-done.2, bf16[1,1536,1536]{2,1,0:T(8,128)(2,1)} %param.16), kind=kOutput, calls=%fused_computation.6 | convolution fusion | flops 3019898880 | bytes 10616832 | tf_op jit(solution)/shard_map/dot_general | solution.py:10
  112.1 6.6 %fusion.2 = f32[640,1536]{1,0:T(8,128)S(1)} fusion(bf16[640,1536]{1,0:T(8,128)(2,1)S(1)} %copy-done.2, bf16[1,1536,1536]{2,1,0:T(8,128)(2,1)} %param.15), kind=kOutput, calls=%fused_computation.2 | convolution fusion | flops 3019898880 | bytes 10616832 | tf_op jit(solution)/shard_map/dot_general | solution.py:10
  118.8 5.4 %multiply_reduce_fusion = (bf16[640]{0:T(1024)(128)(2,1)S(1)}, f32[640,1536]{1,0:T(8,128)}) fusion(f32[640,1536]{1,0:T(8,128)S(1)} %fusion.6, f32[640,1536]{1,0:T(8,128)S(1)} %fusion.2, bf16[640,1536]{1,0:T(8,128)(2,1)S(1)} %copy-done.3, bf16[1,1536,1536]{2,1,0:T(8,128)(2,1)S(1)} %bitcast.64), kind=kOutput, calls=%fused_computation.15 | convolution fusion | flops 3028745728 | bytes 18482432 | tf_op jit(solution)/shard_map/dot_general | solution.py:10
  124.2 0.7 convert_element_type.97
  124.9 3.8 %all-to-all-start.3 = ((bf16[32,1,20]{2,1,0:T(2,128)(2,1)}), bf16[32,1,20]{2,1,0:T(2,128)(2,1)S(1)}, u32[]{:S(2)}, u32[]{:S(2)}) async-start(bf16[32,1,20]{2,1,0:T(2,128)(2,1)} %convert_element_type.97), calls=%async_computation.3 | async-start | bytes 32768 | tf_op jit(solution)/shard_map/all_to_all | solution.py:78
  128.8 8.9 %fusion = f32[640,1536]{1,0:T(8,128)S(1)} fusion(bf16[1,1536,1536]{2,1,0:T(8,128)(2,1)} %param.15, f32[640,1536]{1,0:T(8,128)} %get-tuple-element.12, f32[640,1536]{1,0:T(8,128)} %copy-done.9, f32[640,1536]{1,0:T(8,128)} %copy-done.11), kind=kOutput, calls=%fused_computation | convolution fusion | flops 3031695360 | bytes 20447232 | tf_op jit(solution)/shard_map/dot_general | solution.py:89
  137.7 5.8 %add_convert_fusion = bf16[640,1536]{1,0:T(8,128)(2,1)S(1)} fusion(f32[640,1536]{1,0:T(8,128)S(1)} %fusion, bf16[1,1536,1536]{2,1,0:T(8,128)(2,1)} %param.16, f32[640,1536]{1,0:T(8,128)S(1)} %copy-done.13, f32[640,1536]{1,0:T(8,128)S(1)} %copy-done.10), kind=kOutput, calls=%fused_computation.16 | convolution fusion | flops 3028746240 | bytes 18481152 | tf_op jit(solution)/shard_map/dot_general | solution.py:90
  143.6 2.1 reshape.96
  145.7 7.3 %all-to-all-start.2 = ((bf16[32,20,1536]{2,1,0:T(8,128)(2,1)}), bf16[32,20,1536]{2,1,0:T(8,128)(2,1)S(1)}, u32[]{:S(2)}, u32[]{:S(2)}) async-start(bf16[32,20,1536]{2,1,0:T(8,128)(2,1)} %reshape.96), calls=%async_computation.2 | async-start | bytes 4718592 | tf_op jit(solution)/shard_map/all_to_all | solution.py:78
  154.0 30.6 %all-to-all-done.2 = bf16[32,20,1536]{2,1,0:T(8,128)(2,1)S(1)} async-done(((bf16[32,20,1536]{2,1,0:T(8,128)(2,1)}), bf16[32,20,1536]{2,1,0:T(8,128)(2,1)S(1)}, u32[]{:S(2)}, u32[]{:S(2)}) %all-to-all-start.2) | async-done | bytes 1966112 | tf_op jit(solution)/shard_map/all_to_all | solution.py:78
  184.5 1.5 fusion.19
  186.1 9.9 %fusion.25 = f32[2560,384]{1,0:T(8,128)} fusion(bf16[2560,1536]{1,0:T(8,128)(2,1)} %all-gather.5.cloned.1.call-done, bf16[1,1536,1536]{2,1,0:T(8,128)(2,1)} %param.15, s32[]{:T(128)S(6)} %select_n.2), kind=kOutput, calls=%fused_computation.41 | convolution fusion | flops 3019898880 | bytes 12976132 | tf_op jit(solution)/shard_map/dot_general | solution.py:10
  196.0 7.5 %convolution_add_fusion = f32[2560,384]{1,0:T(8,128)} fusion(bf16[2560,1536]{1,0:T(8,128)(2,1)S(1)} %copy-done.6, bf16[1,1536,1536]{2,1,0:T(8,128)(2,1)} %param.16, s32[]{:T(128)S(6)} %select_n.2), kind=kOutput, calls=%fused_computation.10 | convolution fusion | flops 3020881920 | bytes 12976132 | tf_op jit(solution)/shard_map/dot_general | solution.py:10
  203.4 16.9 %all-gather.3.cloned.1.call-done = bf16[2560,1536]{1,0:T(8,128)(2,1)} async-done(((bf16[640,1536]{1,0:T(8,128)(2,1)}), bf16[2560,1536]{1,0:T(8,128)(2,1)}) %all-gather.3.cloned.1.call-update) | async-done | bytes 7864336 | tf_op jit(solution)/shard_map/all_gather | solution.py:83
  220.3 7.4 %fusion.28 = f32[2560,384]{1,0:T(8,128)S(1)} fusion(bf16[2560,1536]{1,0:T(8,128)(2,1)} %all-gather.3.cloned.1.call-done, bf16[1,1536,1536]{2,1,0:T(8,128)(2,1)} %param.17, s32[]{:T(128)S(6)} %select_n.2), kind=kOutput, calls=%fused_computation.44 | convolution fusion | flops 3019898880 | bytes 12976132 | tf_op jit(solution)/shard_map/dot_general | solution.py:10
  227.7 4.4 %fusion.15 = bf16[1,384,1536]{2,1,0:T(8,128)(2,1)} fusion(bf16[2560,1536]{1,0:T(8,128)(2,1)S(1)} %copy-done.7, f32[2560,384]{1,0:T(8,128)S(1)} %fusion.28, f32[2560,384]{1,0:T(8,128)S(1)} %copy-done.8), kind=kOutput, calls=%fused_computation.28 | convolution fusion | flops 3027369984 | bytes 16908288 | tf_op jit(solution)/shard_map/dot_general | solution.py:16
  232.2 4.5 %fusion.14 = bf16[1,384,1536]{2,1,0:T(8,128)(2,1)} fusion(bf16[2560,1536]{1,0:T(8,128)(2,1)S(1)} %copy-done.7, f32[2560,384]{1,0:T(8,128)S(1)} %fusion.28, f32[2560,384]{1,0:T(8,128)S(1)} %copy-done.12, f32[2560,384]{1,0:T(8,128)S(1)} %copy-done.8), kind=kOutput, calls=%fused_computation.27 | convolution fusion | flops 3031302144 | bytes 20840448 | tf_op jit(solution)/shard_map/dot_general | solution.py:16
  236.7 4.4 %fusion.16 = bf16[1,384,1536]{2,1,0:T(8,128)(2,1)} fusion(bf16[2560,1536]{1,0:T(8,128)(2,1)S(1)} %bitcast.62, f32[2560,384]{1,0:T(8,128)S(1)} %copy-done.12, f32[2560,384]{1,0:T(8,128)S(1)} %copy-done.8), kind=kOutput, calls=%fused_computation.29 | convolution fusion | flops 3027369984 | bytes 16908288 | tf_op jit(solution)/shard_map/dot_general | solution.py:16
  (57 shorter events, 2.3 us)
Async XLA Ops:
  7.2 6.5 %copy-start = (bf16[128,1536]{1,0:T(8,128)(2,1)S(1)}, bf16[128,1536]{1,0:T(8,128)(2,1)}, u32[]{:S(2)}) copy-start(bf16[128,1536]{1,0:T(8,128)(2,1)} %param.10) | copy-start | bytes 1179652
  7.2 178.9 %all-gather.5.cloned.1.call-start = ((), (), s32[]{:S(2)}) async-start(), calls=%async_computation.5 | async-start | bytes 9830400 | tf_op jit(solution)/shard_map/all_gather | solution.py:81
  58.7 4.3 %copy-start.4 = (f32[128,1536]{1,0:T(8,128)S(1)}, f32[128,1536]{1,0:T(8,128)}, u32[]{:S(2)}) copy-start(f32[128,1536]{1,0:T(8,128)} %param.9) | copy-start | bytes 2359300
  62.8 157.5 %all-gather.3.cloned.1.call-start = ((), (), s32[]{:S(2)}) async-start(), calls=%async_computation.4 | async-start | bytes 9830400 | tf_op jit(solution)/shard_map/all_gather | solution.py:83
  102.6 4.2 %copy-start.2 = (bf16[640,1536]{1,0:T(8,128)(2,1)S(1)}, bf16[640,1536]{1,0:T(8,128)(2,1)}, u32[]{:S(2)}) copy-start(bf16[640,1536]{1,0:T(8,128)(2,1)} %reshape.95) | copy-start | bytes 5898244
  106.8 12.0 %slice-start.2 = ((s8[4718592]{0:T(1024)(128)(4,1)}), s8[4194304]{0:T(1024)(128)(4,1)S(1)}, s32[]{:S(2)}) async-start(s8[4718592]{0:T(1024)(128)(4,1)} %bitcast.63), calls=%async_computation.8 | async-start | bytes 8388608
  112.1 6.7 %copy-start.11 = (f32[640,1536]{1,0:T(8,128)}, f32[640,1536]{1,0:T(8,128)S(1)}, u32[]{:S(2)}) copy-start(f32[640,1536]{1,0:T(8,128)S(1)} %fusion.6) | copy-start | bytes 11796484
  112.1 6.7 %copy-start.3 = (bf16[640,1536]{1,0:T(8,128)(2,1)S(1)}, bf16[640,1536]{1,0:T(8,128)(2,1)}, u32[]{:S(2)}) copy-start(bf16[640,1536]{1,0:T(8,128)(2,1)} %reshape.93) | copy-start | bytes 5898244
  112.1 6.7 %slice-start.3 = ((s8[4718592]{0:T(1024)(128)(4,1)}), s8[524288]{0:T(1024)(128)(4,1)S(1)}, s32[]{:S(2)}) async-start(s8[4718592]{0:T(1024)(128)(4,1)} %bitcast.63), calls=%async_computation.9 | async-start | bytes 1048576
  118.8 5.4 %copy-start.9 = (f32[640,1536]{1,0:T(8,128)}, f32[640,1536]{1,0:T(8,128)S(1)}, u32[]{:S(2)}) copy-start(f32[640,1536]{1,0:T(8,128)S(1)} %fusion.2) | copy-start | bytes 11796484
  124.9 20.7 %all-to-all-start.3 = ((bf16[32,1,20]{2,1,0:T(2,128)(2,1)}), bf16[32,1,20]{2,1,0:T(2,128)(2,1)S(1)}, u32[]{:S(2)}, u32[]{:S(2)}) async-start(bf16[32,1,20]{2,1,0:T(2,128)(2,1)} %convert_element_type.97), calls=%async_computation.3 | async-start | bytes 32768 | tf_op jit(solution)/shard_map/all_to_all | solution.py:78
  128.8 9.0 %copy-start.10 = (f32[640,1536]{1,0:T(8,128)S(1)}, f32[640,1536]{1,0:T(8,128)}, u32[]{:S(2)}) copy-start(f32[640,1536]{1,0:T(8,128)} %copy-done.9) | copy-start | bytes 11796484
  128.8 9.0 %copy-start.13 = (f32[640,1536]{1,0:T(8,128)S(1)}, f32[640,1536]{1,0:T(8,128)}, u32[]{:S(2)}) copy-start(f32[640,1536]{1,0:T(8,128)} %get-tuple-element.12) | copy-start | bytes 11796484
  143.6 9.8 %copy-start.5 = (f32[128,4]{0,1:T(4,128)S(1)}, f32[128,4]{0,1:T(4,128)}, u32[]{:S(2)}) copy-start(f32[128,4]{0,1:T(4,128)} %param.11) | copy-start | bytes 6148
  145.7 38.9 %all-to-all-start.2 = ((bf16[32,20,1536]{2,1,0:T(8,128)(2,1)}), bf16[32,20,1536]{2,1,0:T(8,128)(2,1)S(1)}, u32[]{:S(2)}, u32[]{:S(2)}) async-start(bf16[32,20,1536]{2,1,0:T(8,128)(2,1)} %reshape.96), calls=%async_computation.2 | async-start | bytes 4718592 | tf_op jit(solution)/shard_map/all_to_all | solution.py:78
  186.1 9.9 %copy-start.6 = (bf16[2560,1536]{1,0:T(8,128)(2,1)S(1)}, bf16[2560,1536]{1,0:T(8,128)(2,1)}, u32[]{:S(2)}) copy-start(bf16[2560,1536]{1,0:T(8,128)(2,1)} %all-gather.5.cloned.1.call-done) | copy-start | bytes 23592964
  220.3 7.4 %copy-start.7 = (bf16[2560,1536]{1,0:T(8,128)(2,1)S(1)}, bf16[2560,1536]{1,0:T(8,128)(2,1)}, u32[]{:S(2)}) copy-start(bf16[2560,1536]{1,0:T(8,128)(2,1)} %all-gather.5.cloned.1.call-done) | copy-start | bytes 23592964
  220.3 7.4 %copy-start.8 = (f32[2560,384]{1,0:T(8,128)S(1)}, f32[2560,384]{1,0:T(8,128)}, u32[]{:S(2)}) copy-start(f32[2560,384]{1,0:T(8,128)} %fusion.25) | copy-start | bytes 11796484
  227.7 4.5 %copy-start.12 = (f32[2560,384]{1,0:T(8,128)S(1)}, f32[2560,384]{1,0:T(8,128)}, u32[]{:S(2)}) copy-start(f32[2560,384]{1,0:T(8,128)} %convolution_add_fusion) | copy-start | bytes 11796484
  227.7 9.0 %slice-start = ((s8[7864320]{0:T(1024)(128)(4,1)}), s8[4194304]{0:T(1024)(128)(4,1)S(1)}, s32[]{:S(2)}) async-start(s8[7864320]{0:T(1024)(128)(4,1)} %bitcast.61), calls=%async_computation.6 | async-start | bytes 8388608
  232.2 4.6 %slice-start.1 = ((s8[7864320]{0:T(1024)(128)(4,1)}), s8[3670016]{0:T(1024)(128)(4,1)S(1)}, s32[]{:S(2)}) async-start(s8[7864320]{0:T(1024)(128)(4,1)} %bitcast.61), calls=%async_computation.7 | async-start | bytes 7340032
  236.7 4.4 %copy-start.1 = (bf16[128,1536]{1,0:T(8,128)(2,1)S(1)}, bf16[128,1536]{1,0:T(8,128)(2,1)}, u32[]{:S(2)}) copy-start(bf16[128,1536]{1,0:T(8,128)(2,1)} %param.10) | copy-start | bytes 1179652
Sparse Core Ops, SparseCore 0:
  62.9 76.0 all-gather.4
  140.7 79.5 all-gather.2
